TPU v7x, 32 devices: a whole 2x2x4 slice. The times are simulated.
32 devices in a mesh: subj: 8 (over z, core), var: 4 (over y, x).
Axes of the slice: x: 2, y: 2, z: 4, core: 2. Of those that a mesh axis runs over, the one named last changes fastest.
Arguments:
- traits: bfloat16 [16384, 256], P('subj', 'var'), may hold values from -6 to 6
- kin_tiles: bfloat16 [96, 256, 256], P('subj'), may hold values from -0.25 to 0.25
- kin_index: int32 [96, 2], P('subj'), may hold values from 0 to 63, as said below
- dosages: bfloat16 [16384, 3072], P('subj', 'var'), may hold values from 0 to 255, as said below
Outputs:
- scores: float32 [3072, 256], P(('var', 'subj'))
Inputs may be any that keep to these rules, and one draw needn't show every extreme that they name: `kin_index`: rows t * 12 to (t + 1) * 12 - 1 hold tiles whose row block lies in t * 8 to (t + 1) * 8 - 1; every row block has its diagonal tile; counts per row block are uneven; a pair may repeat. `dosages`: whole numbers.
All inputs are finite; a program needn't handle non-finite values.
Results may differ from a plain program's by a relative error of at most 0.009.
Values may be sent and summed in bfloat16 or wider, within the bound.
A program may use at most 64 MiB of HBM per device.

v0:
```python
import jax
import jax.numpy as jnp
from jax import lax
from jax.sharding import PartitionSpec as P


def kinship_apply(field, kin_tiles, kin_index):
    rows_here = field.shape[0]
    block = kin_tiles.shape[1]
    width = field.shape[1]
    blocks_dev = rows_here // block
    gathered = lax.all_gather(field, "subj", axis=0, tiled=True)
    slabs = gathered.reshape(-1, block, width)[kin_index[:, 1]]
    prods = jnp.einsum("tij,tjk->tik", kin_tiles, slabs, preferred_element_type=jnp.float32)
    row_local = kin_index[:, 0] - lax.axis_index("subj") * blocks_dev
    onehot = (row_local[None, :] == jnp.arange(blocks_dev, dtype=jnp.int32)[:, None]).astype(
        jnp.float32
    )
    summed = jnp.einsum("bt,tik->bik", onehot, prods)
    return summed.reshape(rows_here, width)


def on_device(traits, kin_tiles, kin_index, dosages):
    first = kinship_apply(traits, kin_tiles, kin_index)
    first_sent = first.astype(jnp.bfloat16)
    second = kinship_apply(first_sent, kin_tiles, kin_index)
    base = traits.astype(jnp.float32)
    whitened = (0.6 * base + 0.5 * first + 0.3 * (2.0 * second - base)).astype(jnp.bfloat16)
    subjects = traits.shape[0] * lax.axis_size("subj")
    scale = 1.0 / (127.5 * jnp.sqrt(jnp.float32(subjects)))
    contract = (((0,), (0,)), ((), ()))
    wide = lax.all_gather(whitened, "var", axis=1, tiled=True)
    partial_scores = lax.dot_general(dosages, wide, contract, preferred_element_type=jnp.float32)
    scores = lax.psum_scatter(partial_scores, "subj", scatter_dimension=0, tiled=True)
    return scores * scale


def solution(mesh):
    in_specs = (P("subj", "var"), P("subj", None, None), P("subj", None), P("subj", "var"))
    out_specs = P(("var", "subj"), None)
    return jax.shard_map(
        on_device, mesh=mesh, in_specs=in_specs, out_specs=out_specs, check_vma=False
    )
```

profile of v0, /device:TPU:0, one launch (start us, length us, event | category | flops | bytes accessed | tf_op | source)
XLA Modules:
  0.0 159.4 jit_solution(13643037875757538207)
XLA Ops:
  6.5 0.0 copy-start
  6.5 0.0 all-gather.4.cloned.1.call-start
  6.5 0.7 all-gather.4.cloned.1.call-update
  7.3 0.0 all-gather.6.cloned.1.call-start
  7.3 0.9 subtract_bitcast_fusion
  8.2 32.7 %all-gather.4.cloned.1.call-done = bf16[16384,64]{0,1:T(8,128)(2,1)} async-done(((bf16[2048,64]{0,1:T(8,128)(2,1)}), bf16[16384,64]{0,1:T(8,128)(2,1)}) %all-gather.4.cloned.1.call-update) | async-done | bytes 2097168 | tf_op jit(solution)/shard_map/all_gather | solution.py:12
  40.8 3.2 %copy.38 = bf16[8,64,8,256]{3,2,0,1:T(8,128)(2,1)} copy(bf16[8,64,8,256]{3,2,1,0:T(8,128)(2,1)} %bitcast.48) | data formatting | bytes 4194304 | tf_op jit(solution)/shard_map/reshape | solution.py:13
  44.0 2.2 %gather_fusion = bf16[12,256,64]{1,2,0:T(8,128)(2,1)S(1)} fusion(bf16[64,256,64]{1,2,0:T(8,128)(2,1)} %bitcast.44, s32[1024]{0:T(1024)S(1)} %pad_clamp_fusion), kind=kCustom, calls=%fused_computation | custom fusion | bytes 786480 | tf_op jit(solution)/shard_map/gather | solution.py:13
  46.2 2.0 %convolution_bitcast_fusion.2 = bf16[12,256,64]{1,2,0:T(8,128)(2,1)S(1)} fusion(bf16[12,256,64]{1,2,0:T(8,128)(2,1)S(1)} %gather_fusion, bf16[12,256,256]{2,1,0:T(8,128)(2,1)} %param.5), kind=kOutput, calls=%fused_computation.6 | convolution fusion | flops 100663296 | bytes 2359296 | tf_op jit(solution)/shard_map/tij,tjk->tik/dot_general | solution.py:14
  48.2 1.1 fusion.13
  49.3 0.8 copy.27
  50.1 0.0 all-gather.6.cloned.1.call-update
  50.1 0.0 all-gather.8.cloned.1.call-start
  50.2 2.0 %copy.26 = f32[8,8,8,256]{3,1,2,0:T(8,128)} copy(f32[8,8,8,256]{3,2,1,0:T(8,128)} %bitcast.46) | data formatting | bytes 1048576
  52.2 26.6 %all-gather.6.cloned.1.call-done = bf16[16384,64]{0,1:T(8,128)(2,1)} async-done(((bf16[2048,64]{0,1:T(8,128)(2,1)}), bf16[16384,64]{0,1:T(8,128)(2,1)}) %all-gather.6.cloned.1.call-update) | async-done | bytes 2097168 | tf_op jit(solution)/shard_map/all_gather | solution.py:12
  78.8 3.2 %copy.37 = bf16[8,64,8,256]{3,2,0,1:T(8,128)(2,1)} copy(bf16[8,64,8,256]{3,2,1,0:T(8,128)(2,1)} %bitcast.49) | data formatting | bytes 4194304 | tf_op jit(solution)/shard_map/reshape | solution.py:13
  82.0 2.2 %gather_fusion.1 = bf16[12,256,64]{1,2,0:T(8,128)(2,1)S(1)} fusion(bf16[64,256,64]{1,2,0:T(8,128)(2,1)} %bitcast.43, s32[1024]{0:T(1024)S(1)} %pad_clamp_fusion), kind=kCustom, calls=%fused_computation.1 | custom fusion | bytes 786480 | tf_op jit(solution)/shard_map/gather | solution.py:13
  84.2 0.0 copy-start.1
  84.2 0.0 copy-start.2
  84.2 2.1 %convolution_bitcast_fusion.1 = bf16[12,256,64]{1,2,0:T(8,128)(2,1)S(1)} fusion(bf16[12,256,64]{1,2,0:T(8,128)(2,1)S(1)} %gather_fusion.1, bf16[12,256,256]{2,1,0:T(8,128)(2,1)} %param.5), kind=kOutput, calls=%fused_computation.5 | convolution fusion | flops 100663296 | bytes 2359296 | tf_op jit(solution)/shard_map/tij,tjk->tik/dot_general | solution.py:14
  86.3 0.3 convolution_multiply_fusion
  86.6 0.2 copy.28
  86.8 0.0 copy-done.1
  86.8 0.0 copy-done.2
  86.8 0.8 fusion.5
  87.6 0.0 all-gather.8.cloned.1.call-update
  87.7 0.0 reduce-scatter.4.cloned.1.call-start
  87.7 26.0 %all-gather.8.cloned.1.call-done = bf16[2048,256]{0,1:T(8,128)(2,1)} async-done(((bf16[2048,64]{0,1:T(8,128)(2,1)}), bf16[2048,256]{0,1:T(8,128)(2,1)}) %all-gather.8.cloned.1.call-update) | async-done | bytes 1048592 | tf_op jit(solution)/shard_map/all_gather | solution.py:32
  113.7 0.0 copy-done
  113.7 3.1 %convolution_bitcast_fusion = f32[768,256]{0,1:T(8,128)} fusion(bf16[2048,256]{0,1:T(8,128)(2,1)} %all-gather.8.cloned.1.call-done, bf16[2048,768]{1,0:T(8,128)(2,1)S(1)} %copy-done), kind=kOutput, calls=%fused_computation.4 | convolution fusion | flops 805306368 | bytes 4980736 | tf_op jit(solution)/shard_map/dot_general | solution.py:33
  116.9 2.3 %copy.22 = f32[768,256]{1,0:T(8,128)} copy(f32[768,256]{0,1:T(8,128)} %convolution_bitcast_fusion) | data formatting | bytes 1572864
  119.2 0.0 reduce-scatter.4.cloned.1.call-update
  119.2 32.2 %reduce-scatter.4.cloned.1.call-done = f32[96,256]{1,0:T(8,128)} async-done(((f32[768,256]{1,0:T(8,128)}), f32[96,256]{1,0:T(8,128)}) %reduce-scatter.4.cloned.1.call-update) | async-done | bytes 98320 | tf_op jit(solution)/shard_map/reduce_scatter | solution.py:34
  151.4 1.5 broadcast_multiply_fusion.1
  (1 shorter events, 0.0 us)
Async XLA Ops:
  6.5 107.2 %copy-start = (bf16[2048,768]{1,0:T(8,128)(2,1)S(1)}, bf16[2048,768]{1,0:T(8,128)(2,1)}, u32[]{:S(2)}) copy-start(bf16[2048,768]{1,0:T(8,128)(2,1)} %param.7) | copy-start | bytes 9437188
  6.5 34.3 %all-gather.4.cloned.1.call-start = ((), (), s32[]{:S(2)}) async-start(), calls=%async_computation.1 | async-start | bytes 2359296 | tf_op jit(solution)/shard_map/all_gather | solution.py:12
  7.3 71.6 %all-gather.6.cloned.1.call-start = ((), (), s32[]{:S(2)}) async-start(), calls=%async_computation.2 | async-start | bytes 2359296 | tf_op jit(solution)/shard_map/all_gather | solution.py:12
  50.1 63.6 %all-gather.8.cloned.1.call-start = ((), (), s32[]{:S(2)}) async-start(), calls=%async_computation.3 | async-start | bytes 1310720 | tf_op jit(solution)/shard_map/all_gather | solution.py:32
  84.2 2.6 %copy-start.1 = (f32[8,8,8,256]{3,1,2,0:T(8,128)S(1)}, f32[8,8,8,256]{3,1,2,0:T(8,128)}, u32[]{:S(2)}) copy-start(f32[8,8,8,256]{3,1,2,0:T(8,128)} %copy.26) | copy-start | bytes 1572868
  84.2 2.6 %copy-start.2 = (bf16[2048,64]{0,1:T(8,128)(2,1)S(1)}, bf16[2048,64]{0,1:T(8,128)(2,1)}, u32[]{:S(2)}) copy-start(bf16[2048,64]{0,1:T(8,128)(2,1)} %param.4) | copy-start | bytes 786436
  87.7 63.7 %reduce-scatter.4.cloned.1.call-start = ((), (), s32[]{:S(2)}) async-start(), calls=%async_computation.4 | async-start | bytes 884736 | tf_op jit(solution)/shard_map/reduce_scatter | solution.py:34
Sparse Core Ops, SparseCore 0:
  8.9 31.8 all-gather.3
  50.2 28.5 all-gather.5
  87.8 25.8 all-gather.7
  119.3 31.9 reduce-scatter.3
where the time goes:
time: 160 us; the launch traced here: 159 us
  waiting for transfers between devices  118 us (74%)
  local copies, waits for them, and re-layouts  16 us (10%)
  between operations  13.2 us (8%)
  matrix products  8.68 us (5%)
  other arithmetic  3.27 us (2%)
    all_gather x2, waiting for transfers between devices, kinship_apply(): gathered = lax.all_gather(field, 'subj', axis=0, tiled=True)  59.3 us
    reduce_scatter x1, waiting for transfers between devices, on_device(): lax.psum_scatter(partial_scores, 'subj', scatter_dimension=0, tiled=True)  32.2 us
    all_gather x1, waiting for transfers between devices, on_device(): wide = lax.all_gather(whitened, 'var', axis=1, tiled=True)  26 us
    reshape x2, local copies, waits for them, and re-layouts, kinship_apply(): slabs = gathered.reshape(-1, block, width)[kin_index[:, 1]]  6.38 us
    unnamed x10, local copies, waits for them, and re-layouts  5.25 us
    gather x2, local copies, waits for them, and re-layouts, kinship_apply(): slabs = gathered.reshape(-1, block, width)[kin_index[:, 1]]  4.32 us
    dot_general x2, matrix products, kinship_apply(): jnp.einsum('tij,tjk->tik', kin_tiles, slabs, preferred_element_type=jnp.f...  4.08 us
  transfers between devices with their start and end apart: 4, of which 4 were waited for; matrix products, arithmetic and copies ran while one was open for 2% of the time, Pallas kernels for 0%

commit v1 on v0

v1 whole, which is shorter than its diff:
```python
import functools
import math

import jax
import jax.numpy as jnp
from jax import lax
from jax.experimental import pallas as pl
from jax.experimental.pallas import tpu as pltpu
from jax.sharding import PartitionSpec as P

MESH = pl.DeviceIdType.MESH
CORES = 2


def plan_kernel(idx_ref, tab_ref, hot_ref):
    tiles = idx_ref.shape[1]
    blocks, others = hot_ref.shape
    row0 = lax.axis_index("subj") * blocks
    rows = [idx_ref[0, t] - row0 for t in range(tiles)]
    cols = [idx_ref[1, t] for t in range(tiles)]
    zero, one = jnp.int32(0), jnp.int32(1)
    first = []
    for t in range(tiles):
        flag = jnp.where(rows[t] + row0 == cols[t], one, zero)
        for u in range(t):
            flag = flag * jnp.where(rows[u] == rows[t], one - first[u], one)
        first.append(flag)
    for b in range(blocks):
        at = zero
        for t in range(tiles):
            at = at + jnp.where(rows[t] == b, first[t] * t, zero)
        tab_ref[0, b] = at
    ranks = []
    rank = zero
    for t in range(tiles):
        ranks.append(rank)
        rank = rank + (one - first[t])
    for e in range(others):
        tile, row, col = zero, zero, zero
        for t in range(tiles):
            hit = (one - first[t]) * jnp.where(ranks[t] == e, one, zero)
            tile = tile + hit * t
            row = row + hit * rows[t]
            col = col + hit * cols[t]
        tab_ref[1, e] = tile
        tab_ref[2, e] = col
        for b in range(blocks):
            hot_ref[b, e] = jnp.where(row == b, jnp.float32(1), jnp.float32(0))


def kernel(ns, nv, scale, tab_ref, hot_ref, t_ref, tiles_hbm, dos_hbm, o_ref,
           tiles, dos, gat1, gat2, prod, first, wide, part, pbuf, sbuf, rbuf,
           load_sem, zs, zr, ps, pr, ws, wr, qs, qr, rs, rr):
    s, v = lax.axis_index("subj"), lax.axis_index("var")
    nz = ns // CORES
    z, c = s // CORES, s % CORES
    partner = z * CORES + (1 - c)
    nt, blk = tiles.shape[0], tiles.shape[1]
    w, rows_here = t_ref.shape
    nb = rows_here // blk
    ne = nt - nb
    orows = o_ref.shape[0]

    load_t = pltpu.make_async_copy(tiles_hbm, tiles, load_sem.at[0])
    load_d = pltpu.make_async_copy(dos_hbm, dos, load_sem.at[1])
    load_t.start()
    load_d.start()

    barrier = pltpu.get_barrier_semaphore()
    for k in range(1, ns):
        pl.semaphore_signal(barrier, inc=1, device_id={"subj": lax.rem(s + k, ns)}, device_id_type=MESH)
    for k in range(1, nv):
        pl.semaphore_signal(barrier, inc=1, device_id={"var": lax.rem(v + k, nv)}, device_id_type=MESH)
    pl.semaphore_wait(barrier, ns - 1 + nv - 1)

    def gather(phase, gat, meanwhile):
        def blocks(dev):
            return gat.at[pl.ds(dev * nb, nb)]

        def up(k):
            return pltpu.make_async_remote_copy(
                src_ref=blocks(s - k * CORES), dst_ref=blocks(s - k * CORES),
                send_sem=zs.at[phase, 0, k], recv_sem=zr.at[phase, 0, k],
                device_id={"subj": s + CORES}, device_id_type=MESH)

        def down(k):
            return pltpu.make_async_remote_copy(
                src_ref=blocks(s + k * CORES), dst_ref=blocks(s + k * CORES),
                send_sem=zs.at[phase, 1, k], recv_sem=zr.at[phase, 1, k],
                device_id={"subj": s - CORES}, device_id_type=MESH)

        def across(k, sign):
            at = s + sign * k * CORES
            slot = k if sign > 0 else nz - 1 + k
            return pltpu.make_async_remote_copy(
                src_ref=blocks(at), dst_ref=blocks(at),
                send_sem=ps.at[phase, slot], recv_sem=pr.at[phase, slot],
                device_id={"subj": partner}, device_id_type=MESH)

        def landed(at, sem):
            pltpu.make_async_copy(blocks(at), blocks(at), sem).wait()

        @pl.when(z + 1 < nz)
        def _():
            up(0).start()

        @pl.when(z > 0)
        def _():
            down(0).start()

        across(0, 1).start()
        meanwhile()
        for k in range(nz - 1):
            @pl.when(z - 1 - k >= 0)
            def _():
                landed(s - (k + 1) * CORES, zr.at[phase, 0, k])
                if k + 1 < nz - 1:
                    @pl.when(z + 1 < nz)
                    def _():
                        up(k + 1).start()
                across(k + 1, -1).start()

            @pl.when(z + 1 + k < nz)
            def _():
                landed(s + (k + 1) * CORES, zr.at[phase, 1, k])
                if k + 1 < nz - 1:
                    @pl.when(z > 0)
                    def _():
                        down(k + 1).start()
                across(k + 1, 1).start()

        landed(partner, pr.at[phase, 0])
        for k in range(1, nz):
            @pl.when(z - k >= 0)
            def _():
                landed(partner - k * CORES, pr.at[phase, nz - 1 + k])

            @pl.when(z + k < nz)
            def _():
                landed(partner + k * CORES, pr.at[phase, k])

        def finish():
            across(0, 1).wait_send()
            for k in range(1, nz):
                @pl.when(z - k >= 0)
                def _():
                    across(k, -1).wait_send()

                @pl.when(z + k < nz)
                def _():
                    across(k, 1).wait_send()
            for k in range(nz - 1):
                @pl.when((z + 1 < nz) & (z - k >= 0))
                def _():
                    up(k).wait_send()

                @pl.when((z > 0) & (z + k < nz))
                def _():
                    down(k).wait_send()
        return finish

    nt_dims = (((1,), (1,)), ((), ()))

    def apply(field, tile):
        return lax.dot_general(field, tile, nt_dims, preferred_element_type=jnp.float32)

    def diagonals(gat, keep):
        for b in range(nb):
            keep[b] = apply(gat[s * nb + b], tiles[tab_ref[0, b]])

    def off_diagonals(gat):
        for e in range(ne):
            prod[e] = apply(gat[tab_ref[2, e]], tiles[tab_ref[1, e]])

    def total(keep, b):
        value = keep[b]
        for e in range(ne):
            value = value + hot_ref[b, e] * prod[e]
        return value

    for b in range(nb):
        gat1[s * nb + b] = t_ref[:, b * blk:(b + 1) * blk]

    def start1():
        load_t.wait()
        diagonals(gat1, first.at[0])

    finish1 = gather(0, gat1, start1)
    off_diagonals(gat1)
    for b in range(nb):
        value = total(first.at[0], b)
        first[0, b] = value
        gat2[s * nb + b] = value.astype(jnp.bfloat16)

    finish2 = gather(1, gat2, lambda: diagonals(gat2, first.at[1]))
    off_diagonals(gat2)
    mine = wide.at[pl.ds(pl.multiple_of(v * w, w), w)]
    for b in range(nb):
        at = slice(b * blk, (b + 1) * blk)
        base = t_ref[:, at].astype(jnp.float32)
        second = total(first.at[1], b)
        mine[:, at] = (
            0.6 * base + 0.5 * first[0, b] + 0.3 * (2.0 * second - base)
        ).astype(jnp.bfloat16)

    sends = []
    for k in range(1, nv):
        sends.append(pltpu.make_async_remote_copy(
            src_ref=mine, dst_ref=mine, send_sem=ws.at[k], recv_sem=wr.at[k],
            device_id={"var": lax.rem(v + k, nv)}, device_id_type=MESH))
        sends[-1].start()
    finish1()
    finish2()
    load_d.wait()
    for k in range(1, nv):
        sends[k - 1].wait()

    for lo in range(0, dos.shape[1], blk):
        got = jnp.dot(wide[...], dos[:, lo:lo + blk], preferred_element_type=jnp.float32)
        part[lo:lo + blk, :] = got.T

    pairs = []
    for q in range(nz):
        pairs.append(pltpu.make_async_remote_copy(
            src_ref=part.at[pl.ds((q * CORES + 1 - c) * orows, orows)], dst_ref=pbuf.at[q],
            send_sem=qs.at[q], recv_sem=qr.at[q],
            device_id={"subj": partner}, device_id_type=MESH))
        pairs[-1].start()
    for q in range(nz):
        pairs[q].wait()
    outs = []
    for k in range(1, nz):
        to = lax.rem(z + k, nz)
        sbuf[k] = (part[pl.ds((to * CORES + c) * orows, orows), :] + pbuf[to]).astype(jnp.bfloat16)
        outs.append(pltpu.make_async_remote_copy(
            src_ref=sbuf.at[k], dst_ref=rbuf.at[k], send_sem=rs.at[k], recv_sem=rr.at[k],
            device_id={"subj": to * CORES + c}, device_id_type=MESH))
        outs[-1].start()
    acc = part[pl.ds(s * orows, orows), :] + pbuf[z]
    for k in range(1, nz):
        outs[k - 1].wait()
        acc = acc + rbuf[k].astype(jnp.float32)
    o_ref[...] = acc * scale


def on_device(ns, nv, traits, kin_tiles, kin_index, dosages):
    rows_here, w = traits.shape
    nt, blk = kin_tiles.shape[:2]
    nb = rows_here // blk
    ne = nt - nb
    nz = ns // CORES
    var_dev = dosages.shape[1]
    orows = var_dev // ns
    k_all = w * nv
    bf16, f32 = jnp.bfloat16, jnp.float32
    dma = pltpu.SemaphoreType.DMA
    scale = 1.0 / (127.5 * math.sqrt(rows_here * ns))
    any_spec = pl.BlockSpec(memory_space=pl.ANY)
    vmem = pl.BlockSpec(memory_space=pltpu.VMEM)
    smem = pl.BlockSpec(memory_space=pltpu.SMEM)
    tab, hot = pl.pallas_call(
        plan_kernel,
        out_shape=(jax.ShapeDtypeStruct((3, max(nb, ne)), jnp.int32),
                   jax.ShapeDtypeStruct((nb, ne), f32)),
        in_specs=[smem],
        out_specs=(smem, smem),
    )(kin_index.T)
    return pl.pallas_call(
        functools.partial(kernel, ns, nv, scale),
        out_shape=jax.ShapeDtypeStruct((orows, k_all), f32),
        in_specs=[smem, smem, vmem, any_spec, any_spec],
        out_specs=vmem,
        scratch_shapes=[
            pltpu.VMEM((nt, blk, blk), bf16),
            pltpu.VMEM((rows_here, var_dev), bf16),
            pltpu.VMEM((ns * nb, w, blk), bf16),
            pltpu.VMEM((ns * nb, w, blk), bf16),
            pltpu.VMEM((ne, w, blk), f32),
            pltpu.VMEM((2, nb, w, blk), f32),
            pltpu.VMEM((k_all, rows_here), bf16),
            pltpu.VMEM((var_dev, k_all), f32),
            pltpu.VMEM((nz, orows, k_all), f32),
            pltpu.VMEM((nz, orows, k_all), bf16),
            pltpu.VMEM((nz, orows, k_all), bf16),
            dma((2,)),
            dma((2, 2, nz)), dma((2, 2, nz)),
            dma((2, 2 * nz)), dma((2, 2 * nz)),
            dma((nv,)), dma((nv,)),
            dma((nz,)), dma((nz,)),
            dma((nz,)), dma((nz,)),
        ],
        compiler_params=pltpu.CompilerParams(
            collective_id=0, has_side_effects=True, vmem_limit_bytes=60 * 1024 * 1024),
    )(tab, hot, traits.T, kin_tiles, dosages)


def solution(mesh):
    in_specs = (P("subj", "var"), P("subj", None, None), P("subj", None), P("subj", "var"))
    out_specs = P(("var", "subj"), None)
    body = functools.partial(on_device, mesh.shape["subj"], mesh.shape["var"])
    return jax.shard_map(
        body, mesh=mesh, in_specs=in_specs, out_specs=out_specs, check_vma=False
    )
```

time: 160 us -> 79.3 us (0.50)
  waiting for transfers between devices: 118 us -> 0 us
  Pallas kernels: 0 us -> 77.6 us
  local copies, waits for them, and re-layouts: 16 us -> 1.54 us
  between operations: 13.2 us -> 0.02 us
  matrix products: 8.68 us -> 0 us
  other arithmetic: 3.27 us -> 0 us
    all_gather x3 -> x0, waiting for transfers between devices: 85.3 us -> none  [the longest x2 59.3 us: kinship_apply(): gathered = lax.all_gather(field, 'subj', axis=0, tiled=True)]
    pallas_call x0 -> x2, Pallas kernels: none -> 77.6 us  [the longest x1 75.8 us: on_device(): pl.pallas_call(functools.partial(kernel, ns, nv, scale), out_shape=jax.Sh...]
    reduce_scatter x1 -> x0, waiting for transfers between devices: 32.2 us -> none  [on_device(): lax.psum_scatter(partial_scores, 'subj', scatter_dimension=0, tiled=True)]
    dot_general x5 -> x0, matrix products: 8.68 us -> none  [the longest x2 4.08 us: kinship_apply(): jnp.einsum('tij,tjk->tik', kin_tiles, slabs, preferred_element_type=jnp.f...]
    reshape x2 -> x0, local copies, waits for them, and re-layouts: 6.38 us -> none  [kinship_apply(): slabs = gathered.reshape(-1, block, width)[kin_index[:, 1]]]
    gather x2 -> x0, local copies, waits for them, and re-layouts: 4.32 us -> none  [kinship_apply(): slabs = gathered.reshape(-1, block, width)[kin_index[:, 1]]]
    unnamed x10 -> x1, local copies, waits for them, and re-layouts: 5.25 us -> 1.54 us
  transfers between devices with their start and end apart: 4 -> 0, of which waited for: 4 -> 0; matrix products, arithmetic and copies ran while one was open for 2% -> 0% of each run, Pallas kernels for 0% -> 0%
where the time goes in v1:
time: 79.3 us; the launch traced here: 79.1 us
  Pallas kernels  77.6 us (98%)
  local copies, waits for them, and re-layouts  1.54 us (2%)
    pallas_call x1, Pallas kernels, on_device(): pl.pallas_call(functools.partial(kernel, ns, nv, scale), out_shape=jax.Sh...  75.8 us
    pallas_call x1, Pallas kernels, on_device(): pl.pallas_call(plan_kernel, out_shape=(jax.ShapeDtypeStruct((3, max(nb, n...  1.75 us

profile of v1, /device:TPU:0, one launch (start us, length us, event | category | flops | bytes accessed | tf_op | source)
XLA Modules:
  0.0 79.1 jit_solution(11483243858941944950)
XLA Ops:
  0.0 1.7 %shard_map.46 = (s32[3,8]{1,0:T(4,128)}, f32[8,4]{1,0:T(8,128)}) custom-call(s32[2,12]{1,0:T(2,128)} %bitcast.3), custom_call_target="tpu_custom_call" | custom-call | tf_op jit(solution)/shard_map/pallas_call | solution.py:261
  1.8 75.8 %shard_map.47 = f32[96,256]{1,0:T(8,128)} custom-call(s32[3,8]{1,0:T(4,128)} %get-tuple-element.7.tab_ref, f32[8,4]{1,0:T(8,128)} %get-tuple-element.8.hot_ref, bf16[64,2048]{1,0:T(8,128)(2,1)} %bitcast.2, bf16[12,256,256]{2,1,0:T(8,128)(2,1)} %tiles_hbm.1, bf16[2048,768]{1,0:T(8,128)(2,1)} %dos_hbm.1), custom_call_target="tpu_custom_call" | custom-call | tf_op jit(solution)/shard_map/pallas_call | solution.py:268
  77.6 1.5 %copy.6 = f32[96,256]{1,0:T(8,128)} copy(f32[96,256]{1,0:T(8,128)} %shard_map.47) | data formatting | bytes 196608

commit v2 on v1

--- a/solution.py
+++ b/solution.py
@@ -49,7 +49,7 @@
 
 
 def kernel(ns, nv, scale, tab_ref, hot_ref, t_ref, tiles_hbm, dos_hbm, o_ref,
-           tiles, dos, gat1, gat2, prod, first, wide, part, pbuf, sbuf, rbuf,
+           tiles, dos, turned, gat1, gat2, prod, first, wide, part, pbuf, sbuf, rbuf,
            load_sem, zs, zr, ps, pr, ws, wr, qs, qr, rs, rr):
     s, v = lax.axis_index("subj"), lax.axis_index("var")
     nz = ns // CORES
@@ -60,6 +60,7 @@
     nb = rows_here // blk
     ne = nt - nb
     orows = o_ref.shape[0]
+    var_dev = dos.shape[1]
 
     load_t = pltpu.make_async_copy(tiles_hbm, tiles, load_sem.at[0])
     load_d = pltpu.make_async_copy(dos_hbm, dos, load_sem.at[1])
@@ -67,96 +68,72 @@
     load_d.start()
 
     barrier = pltpu.get_barrier_semaphore()
-    for k in range(1, ns):
-        pl.semaphore_signal(barrier, inc=1, device_id={"subj": lax.rem(s + k, ns)}, device_id_type=MESH)
+    pl.semaphore_signal(barrier, inc=1, device_id={"subj": partner}, device_id_type=MESH)
+    for k in range(1, nz):
+        pl.semaphore_signal(
+            barrier, inc=1, device_id={"subj": lax.rem(z + k, nz) * CORES + c}, device_id_type=MESH)
     for k in range(1, nv):
         pl.semaphore_signal(barrier, inc=1, device_id={"var": lax.rem(v + k, nv)}, device_id_type=MESH)
-    pl.semaphore_wait(barrier, ns - 1 + nv - 1)
-
-    def gather(phase, gat, meanwhile):
-        def blocks(dev):
-            return gat.at[pl.ds(dev * nb, nb)]
-
-        def up(k):
+    pl.semaphore_wait(barrier, 1 + nz - 1 + nv - 1)
+
+    def turn(off):
+        return lax.rem(z + off + nz, nz) * CORES
+
+    def gather(phase, gat, meanwhile, later=lambda: None):
+        parts = ((0, nb // 2), (nb // 2, nb - nb // 2))
+
+        def piece(dev, half):
+            return gat.at[pl.ds(dev * nb + parts[half][0], parts[half][1])]
+
+        def hop(sign, dist, half):
+            ref = piece(turn(-sign * (dist - 1)) + c, half)
+            way = 0 if sign > 0 else 1
             return pltpu.make_async_remote_copy(
-                src_ref=blocks(s - k * CORES), dst_ref=blocks(s - k * CORES),
-                send_sem=zs.at[phase, 0, k], recv_sem=zr.at[phase, 0, k],
-                device_id={"subj": s + CORES}, device_id_type=MESH)
-
-        def down(k):
+                src_ref=ref, dst_ref=ref,
+                send_sem=zs.at[phase, way, dist, half], recv_sem=zr.at[phase, way, dist, half],
+                device_id={"subj": turn(sign) + c}, device_id_type=MESH)
+
+        def across(off, half):
+            ref = piece(turn(off) + c, half)
             return pltpu.make_async_remote_copy(
-                src_ref=blocks(s + k * CORES), dst_ref=blocks(s + k * CORES),
-                send_sem=zs.at[phase, 1, k], recv_sem=zr.at[phase, 1, k],
-                device_id={"subj": s - CORES}, device_id_type=MESH)
-
-        def across(k, sign):
-            at = s + sign * k * CORES
-            slot = k if sign > 0 else nz - 1 + k
-            return pltpu.make_async_remote_copy(
-                src_ref=blocks(at), dst_ref=blocks(at),
-                send_sem=ps.at[phase, slot], recv_sem=pr.at[phase, slot],
+                src_ref=ref, dst_ref=ref,
+                send_sem=ps.at[phase, off % nz, half], recv_sem=pr.at[phase, off % nz, half],
                 device_id={"subj": partner}, device_id_type=MESH)
 
-        def landed(at, sem):
-            pltpu.make_async_copy(blocks(at), blocks(at), sem).wait()
-
-        @pl.when(z + 1 < nz)
-        def _():
-            up(0).start()
-
-        @pl.when(z > 0)
-        def _():
-            down(0).start()
-
-        across(0, 1).start()
+        def landed(dev, half, sem):
+            ref = piece(dev, half)
+            pltpu.make_async_copy(ref, ref, sem).wait()
+
+        steps = []
+        for dist in range(1, nz // 2 + 1):
+            if 2 * dist < nz:
+                steps += [(1, dist, 0), (-1, dist, 1), (1, dist, 1), (-1, dist, 0)]
+            else:
+                steps += [(1, dist, 0), (-1, dist, 1)]
+        for step in steps:
+            if step[1] == 1:
+                hop(*step).start()
+        for half in range(2):
+            across(0, half).start()
         meanwhile()
-        for k in range(nz - 1):
-            @pl.when(z - 1 - k >= 0)
-            def _():
-                landed(s - (k + 1) * CORES, zr.at[phase, 0, k])
-                if k + 1 < nz - 1:
-                    @pl.when(z + 1 < nz)
-                    def _():
-                        up(k + 1).start()
-                across(k + 1, -1).start()
-
-            @pl.when(z + 1 + k < nz)
-            def _():
-                landed(s + (k + 1) * CORES, zr.at[phase, 1, k])
-                if k + 1 < nz - 1:
-                    @pl.when(z > 0)
-                    def _():
-                        down(k + 1).start()
-                across(k + 1, 1).start()
-
-        landed(partner, pr.at[phase, 0])
-        for k in range(1, nz):
-            @pl.when(z - k >= 0)
-            def _():
-                landed(partner - k * CORES, pr.at[phase, nz - 1 + k])
-
-            @pl.when(z + k < nz)
-            def _():
-                landed(partner + k * CORES, pr.at[phase, k])
+        for i, (sign, dist, half) in enumerate(steps):
+            way = 0 if sign > 0 else 1
+            landed(turn(-sign * dist) + c, half, zr.at[phase, way, dist, half])
+            if (sign, dist + 1, half) in steps:
+                hop(sign, dist + 1, half).start()
+            across(-sign * dist, half).start()
+            if i == 1:
+                later()
+        for off in range(nz):
+            for half in range(2):
+                landed(turn(off) + 1 - c, half, pr.at[phase, off, half])
 
         def finish():
-            across(0, 1).wait_send()
-            for k in range(1, nz):
-                @pl.when(z - k >= 0)
-                def _():
-                    across(k, -1).wait_send()
-
-                @pl.when(z + k < nz)
-                def _():
-                    across(k, 1).wait_send()
-            for k in range(nz - 1):
-                @pl.when((z + 1 < nz) & (z - k >= 0))
-                def _():
-                    up(k).wait_send()
-
-                @pl.when((z > 0) & (z + k < nz))
-                def _():
-                    down(k).wait_send()
+            for off in range(nz):
+                for half in range(2):
+                    across(off, half).wait_send()
+            for step in steps:
+                hop(*step).wait_send()
         return finish
 
     nt_dims = (((1,), (1,)), ((), ()))
@@ -192,32 +169,31 @@
         first[0, b] = value
         gat2[s * nb + b] = value.astype(jnp.bfloat16)
 
-    finish2 = gather(1, gat2, lambda: diagonals(gat2, first.at[1]))
+    def turn_dosages():
+        load_d.wait()
+        for lo in range(0, var_dev, blk):
+            for b in range(nb):
+                turned[lo:lo + blk, b * blk:(b + 1) * blk] = dos[b * blk:(b + 1) * blk, lo:lo + blk].T
+
+    finish2 = gather(1, gat2, lambda: diagonals(gat2, first.at[1]), turn_dosages)
     off_diagonals(gat2)
-    mine = wide.at[pl.ds(pl.multiple_of(v * w, w), w)]
-    for b in range(nb):
-        at = slice(b * blk, (b + 1) * blk)
-        base = t_ref[:, at].astype(jnp.float32)
-        second = total(first.at[1], b)
-        mine[:, at] = (
-            0.6 * base + 0.5 * first[0, b] + 0.3 * (2.0 * second - base)
-        ).astype(jnp.bfloat16)
-
+    spans = ((0, nb // 2), (nb // 2, nb))
+    row_v = pl.ds(pl.multiple_of(v * w, w), w)
     sends = []
-    for k in range(1, nv):
-        sends.append(pltpu.make_async_remote_copy(
-            src_ref=mine, dst_ref=mine, send_sem=ws.at[k], recv_sem=wr.at[k],
-            device_id={"var": lax.rem(v + k, nv)}, device_id_type=MESH))
-        sends[-1].start()
-    finish1()
-    finish2()
-    load_d.wait()
-    for k in range(1, nv):
-        sends[k - 1].wait()
-
-    for lo in range(0, dos.shape[1], blk):
-        got = jnp.dot(wide[...], dos[:, lo:lo + blk], preferred_element_type=jnp.float32)
-        part[lo:lo + blk, :] = got.T
+    for i, (b0, b1) in enumerate(spans):
+        for b in range(b0, b1):
+            at = slice(b * blk, (b + 1) * blk)
+            base = t_ref[:, at].astype(jnp.float32)
+            second = total(first.at[1], b)
+            wide[row_v, at] = (
+                0.6 * base + 0.5 * first[0, b] + 0.3 * (2.0 * second - base)
+            ).astype(jnp.bfloat16)
+        mine = wide.at[row_v, pl.ds(b0 * blk, (b1 - b0) * blk)]
+        for k in range(1, nv):
+            sends.append(pltpu.make_async_remote_copy(
+                src_ref=mine, dst_ref=mine, send_sem=ws.at[i, k], recv_sem=wr.at[i, k],
+                device_id={"var": lax.rem(v + k, nv)}, device_id_type=MESH))
+            sends[-1].start()
 
     pairs = []
     for q in range(nz):
@@ -225,7 +201,23 @@
             src_ref=part.at[pl.ds((q * CORES + 1 - c) * orows, orows)], dst_ref=pbuf.at[q],
             send_sem=qs.at[q], recv_sem=qr.at[q],
             device_id={"subj": partner}, device_id_type=MESH))
-        pairs[-1].start()
+    sent = 0
+    for i, (b0, b1) in enumerate(spans):
+        for k in range(1, nv):
+            sends[i * (nv - 1) + k - 1].wait_recv()
+        for lo in range(0, var_dev, blk):
+            got = apply(turned[lo:lo + blk, b0 * blk:b1 * blk], wide[:, b0 * blk:b1 * blk])
+            if i == 0:
+                part[lo:lo + blk, :] = got
+                continue
+            part[lo:lo + blk, :] += got
+            while sent < nz and (sent + 1) * CORES * orows <= lo + blk:
+                pairs[sent].start()
+                sent += 1
+    finish1()
+    finish2()
+    for copy in sends:
+        copy.wait_send()
     for q in range(nz):
         pairs[q].wait()
     outs = []
@@ -273,6 +265,7 @@
         scratch_shapes=[
             pltpu.VMEM((nt, blk, blk), bf16),
             pltpu.VMEM((rows_here, var_dev), bf16),
+            pltpu.VMEM((var_dev, rows_here), bf16),
             pltpu.VMEM((ns * nb, w, blk), bf16),
             pltpu.VMEM((ns * nb, w, blk), bf16),
             pltpu.VMEM((ne, w, blk), f32),
@@ -283,9 +276,9 @@
             pltpu.VMEM((nz, orows, k_all), bf16),
             pltpu.VMEM((nz, orows, k_all), bf16),
             dma((2,)),
-            dma((2, 2, nz)), dma((2, 2, nz)),
-            dma((2, 2 * nz)), dma((2, 2 * nz)),
-            dma((nv,)), dma((nv,)),
+            dma((2, 2, nz, 2)), dma((2, 2, nz, 2)),
+            dma((2, nz, 2)), dma((2, nz, 2)),
+            dma((2, nv)), dma((2, nv)),
             dma((nz,)), dma((nz,)),
             dma((nz,)), dma((nz,)),
         ],

time: 79.3 us -> 73.5 us (0.927)
  Pallas kernels: 77.6 us -> 71.8 us
    pallas_call x1, Pallas kernels: 75.8 us -> 70 us  [on_device(): pl.pallas_call(functools.partial(kernel, ns, nv, scale), out_shape=jax.Sh...]
where the time goes in v2:
time: 73.5 us; the launch traced here: 73.3 us
  Pallas kernels  71.8 us (98%)
  local copies, waits for them, and re-layouts  1.54 us (2%)
    pallas_call x1, Pallas kernels, on_device(): pl.pallas_call(functools.partial(kernel, ns, nv, scale), out_shape=jax.Sh...  70 us
    pallas_call x1, Pallas kernels, on_device(): pl.pallas_call(plan_kernel, out_shape=(jax.ShapeDtypeStruct((3, max(nb, n...  1.75 us
    unnamed x1, local copies, waits for them, and re-layouts  1.54 us

profile of v2, /device:TPU:0, one launch (start us, length us, event | category | flops | bytes accessed | tf_op | source)
XLA Modules:
  0.0 73.3 jit_solution(16916160114867324663)
XLA Ops:
  0.0 1.7 %shard_map.46 = (s32[3,8]{1,0:T(4,128)}, f32[8,4]{1,0:T(8,128)}) custom-call(s32[2,12]{1,0:T(2,128)} %bitcast.3), custom_call_target="tpu_custom_call" | custom-call | tf_op jit(solution)/shard_map/pallas_call | solution.py:253
  1.8 70.0 %shard_map.47 = f32[96,256]{1,0:T(8,128)} custom-call(s32[3,8]{1,0:T(4,128)} %get-tuple-element.7.tab_ref, f32[8,4]{1,0:T(8,128)} %get-tuple-element.8.hot_ref, bf16[64,2048]{1,0:T(8,128)(2,1)} %bitcast.2, bf16[12,256,256]{2,1,0:T(8,128)(2,1)} %tiles_hbm.1, bf16[2048,768]{1,0:T(8,128)(2,1)} %dos_hbm.1), custom_call_target="tpu_custom_call" | custom-call | tf_op jit(solution)/shard_map/pallas_call | solution.py:260
  71.8 1.5 %copy.6 = f32[96,256]{1,0:T(8,128)} copy(f32[96,256]{1,0:T(8,128)} %shard_map.47) | data formatting | bytes 196608

commit v3 on v2

--- a/solution.py
+++ b/solution.py
@@ -35,6 +35,7 @@
     for t in range(tiles):
         ranks.append(rank)
         rank = rank + (one - first[t])
+    touched = [zero] * blocks
     for e in range(others):
         tile, row, col = zero, zero, zero
         for t in range(tiles):
@@ -46,6 +47,16 @@
         tab_ref[2, e] = col
         for b in range(blocks):
             hot_ref[b, e] = jnp.where(row == b, jnp.float32(1), jnp.float32(0))
+            touched[b] = jnp.where(row == b, one, touched[b])
+    late = zero
+    for b in range(blocks):
+        late = late + touched[b]
+    early_at, late_at = zero, blocks - late
+    for b in range(blocks):
+        slot = jnp.where(touched[b] == one, late_at, early_at)
+        tab_ref[3, slot] = jnp.int32(b)
+        late_at = late_at + touched[b]
+        early_at = early_at + (one - touched[b])
 
 
 def kernel(ns, nv, scale, tab_ref, hot_ref, t_ref, tiles_hbm, dos_hbm, o_ref,
@@ -60,7 +71,7 @@
     nb = rows_here // blk
     ne = nt - nb
     orows = o_ref.shape[0]
-    var_dev = dos.shape[1]
+    var_dev = dos.shape[2]
 
     load_t = pltpu.make_async_copy(tiles_hbm, tiles, load_sem.at[0])
     load_d = pltpu.make_async_copy(dos_hbm, dos, load_sem.at[1])
@@ -173,27 +184,37 @@
         load_d.wait()
         for lo in range(0, var_dev, blk):
             for b in range(nb):
-                turned[lo:lo + blk, b * blk:(b + 1) * blk] = dos[b * blk:(b + 1) * blk, lo:lo + blk].T
-
-    finish2 = gather(1, gat2, lambda: diagonals(gat2, first.at[1]), turn_dosages)
-    off_diagonals(gat2)
-    spans = ((0, nb // 2), (nb // 2, nb))
+                turned[lo:lo + blk, b * blk:(b + 1) * blk] = dos[tab_ref[3, b], :, lo:lo + blk].T
+
+    early = max(nb - ne, 0)
+    spans = [span for span in ((0, early), (early, nb)) if span[0] < span[1]]
     row_v = pl.ds(pl.multiple_of(v * w, w), w)
     sends = []
-    for i, (b0, b1) in enumerate(spans):
-        for b in range(b0, b1):
-            at = slice(b * blk, (b + 1) * blk)
-            base = t_ref[:, at].astype(jnp.float32)
-            second = total(first.at[1], b)
-            wide[row_v, at] = (
+
+    def whiten(b0, b1):
+        for j in range(b0, b1):
+            b = tab_ref[3, j]
+            base = gat1[s * nb + b].astype(jnp.float32)
+            second = first[1, b] if b1 <= early else total(first.at[1], b)
+            wide[row_v, j * blk:(j + 1) * blk] = (
                 0.6 * base + 0.5 * first[0, b] + 0.3 * (2.0 * second - base)
             ).astype(jnp.bfloat16)
         mine = wide.at[row_v, pl.ds(b0 * blk, (b1 - b0) * blk)]
+        i = len(sends) // (nv - 1) if nv > 1 else 0
         for k in range(1, nv):
             sends.append(pltpu.make_async_remote_copy(
                 src_ref=mine, dst_ref=mine, send_sem=ws.at[i, k], recv_sem=wr.at[i, k],
                 device_id={"var": lax.rem(v + k, nv)}, device_id_type=MESH))
             sends[-1].start()
+
+    def start2():
+        diagonals(gat2, first.at[1])
+        if early:
+            whiten(0, early)
+
+    finish2 = gather(1, gat2, start2, turn_dosages)
+    off_diagonals(gat2)
+    whiten(early, nb)
 
     pairs = []
     for q in range(nz):
@@ -207,10 +228,9 @@
             sends[i * (nv - 1) + k - 1].wait_recv()
         for lo in range(0, var_dev, blk):
             got = apply(turned[lo:lo + blk, b0 * blk:b1 * blk], wide[:, b0 * blk:b1 * blk])
-            if i == 0:
-                part[lo:lo + blk, :] = got
+            part[lo:lo + blk, :] = got if i == 0 else part[lo:lo + blk, :] + got
+            if i + 1 < len(spans):
                 continue
-            part[lo:lo + blk, :] += got
             while sent < nz and (sent + 1) * CORES * orows <= lo + blk:
                 pairs[sent].start()
                 sent += 1
@@ -252,7 +272,7 @@
     smem = pl.BlockSpec(memory_space=pltpu.SMEM)
     tab, hot = pl.pallas_call(
         plan_kernel,
-        out_shape=(jax.ShapeDtypeStruct((3, max(nb, ne)), jnp.int32),
+        out_shape=(jax.ShapeDtypeStruct((4, max(nb, ne)), jnp.int32),
                    jax.ShapeDtypeStruct((nb, ne), f32)),
         in_specs=[smem],
         out_specs=(smem, smem),
@@ -264,7 +284,7 @@
         out_specs=vmem,
         scratch_shapes=[
             pltpu.VMEM((nt, blk, blk), bf16),
-            pltpu.VMEM((rows_here, var_dev), bf16),
+            pltpu.VMEM((nb, blk, var_dev), bf16),
             pltpu.VMEM((var_dev, rows_here), bf16),
             pltpu.VMEM((ns * nb, w, blk), bf16),
             pltpu.VMEM((ns * nb, w, blk), bf16),
@@ -284,7 +304,7 @@
         ],
         compiler_params=pltpu.CompilerParams(
             collective_id=0, has_side_effects=True, vmem_limit_bytes=60 * 1024 * 1024),
-    )(tab, hot, traits.T, kin_tiles, dosages)
+    )(tab, hot, traits.T, kin_tiles, dosages.reshape(nb, blk, var_dev))
 
 
 def solution(mesh):

time: 73.5 us -> 67.9 us (0.924)
  Pallas kernels: 71.8 us -> 66.2 us
    pallas_call x1, Pallas kernels: 70 us -> 64.3 us  [on_device(): pl.pallas_call(functools.partial(kernel, ns, nv, scale), out_shape=jax.Sh...]
where the time goes in v3:
time: 67.9 us; the launch traced here: 67.7 us
  Pallas kernels  66.2 us (97%)
  local copies, waits for them, and re-layouts  1.54 us (2%)
    pallas_call x1, Pallas kernels, on_device(): pl.pallas_call(functools.partial(kernel, ns, nv, scale), out_shape=jax.Sh...  64.3 us
    pallas_call x1, Pallas kernels, on_device(): pl.pallas_call(plan_kernel, out_shape=(jax.ShapeDtypeStruct((4, max(nb, n...  1.82 us
    unnamed x1, local copies, waits for them, and re-layouts  1.54 us

profile of v3, /device:TPU:0, one launch (start us, length us, event | category | flops | bytes accessed | tf_op | source)
XLA Modules:
  0.0 67.7 jit_solution(4120807201221493329)
XLA Ops:
  0.0 1.8 %shard_map.46 = (s32[4,8]{1,0:T(4,128)}, f32[8,4]{1,0:T(8,128)}) custom-call(s32[2,12]{1,0:T(2,128)} %bitcast.5), custom_call_target="tpu_custom_call" | custom-call | tf_op jit(solution)/shard_map/pallas_call | solution.py:273
  1.8 64.3 %shard_map.47 = f32[96,256]{1,0:T(8,128)} custom-call(s32[4,8]{1,0:T(4,128)} %get-tuple-element.7.tab_ref, f32[8,4]{1,0:T(8,128)} %get-tuple-element.8.hot_ref, bf16[64,2048]{1,0:T(8,128)(2,1)} %bitcast.4, bf16[12,256,256]{2,1,0:T(8,128)(2,1)} %tiles_hbm.1, bf16[8,256,768]{2,1,0:T(8,128)(2,1)} %bitcast.3), custom_call_target="tpu_custom_call" | custom-call | tf_op jit(solution)/shard_map/pallas_call | solution.py:280
  66.2 1.5 %copy.6 = f32[96,256]{1,0:T(8,128)} copy(f32[96,256]{1,0:T(8,128)} %shard_map.47) | data formatting | bytes 196608
